TPU v7x, 256 devices: a 8x8x2 block of a 8x8x16 slice. The times are simulated.
256 devices in a mesh: groups: 2 (over z), expert: 16 (over x, core), cuts: 8 (over y).
Axes of the slice: x: 8, y: 8, z: 2, core: 2. Of those that a mesh axis runs over, the one named last changes fastest.
The devices are a block of a 8x8x16 slice.
Arguments:
- tokens: bfloat16 [16384, 2048], P(('groups', 'expert')), parts along dimension 0, may hold values from -6 to 6
- route: int32 [16384, 1], P(('groups', 'expert')), parts along dimension 0, may hold values from 0 to 15; in each aligned block of 512 rows (0 to 511, 512 to 1023, ...) at most 48 rows name the same one
- gate_prob: float32 [16384], P(('groups', 'expert')), parts along dimension 0, may hold values from 0.2 to 1
- norm_gain: float32 [2048], replicated, may hold values from 0.5 to 1.5
- dense_in: bfloat16 [2048, 8192], P('expert', 'cuts'), may hold values from -0.125 to 0.125
- dense_out: bfloat16 [8192, 2048], P('cuts', 'expert'), may hold values from -0.0625 to 0.0625
- expert_in: bfloat16 [16, 2048, 8192], P('expert', None, 'cuts'), may hold values from -0.125 to 0.125
- expert_out: bfloat16 [16, 8192, 2048], P('expert', 'cuts'), may hold values from -0.0625 to 0.0625
Outputs:
- layer_out: bfloat16 [16384, 2048], P(('groups', 'expert'), 'cuts'), parts along dimension 0
There are 2 independent parts, one for each index of `groups`. A program takes and returns all parts, laid end to end along the dimension named above; an argument that names none is the same for every part. Nothing has to cross between parts.
Inputs may be any that keep to these rules, and one draw needn't show every extreme that they name: `route`: within the rows of one device (aligned blocks of 512 rows) no expert is named by more than 48 rows; in some blocks one expert is named by exactly 48 rows.
All inputs are finite; a program needn't handle non-finite values.
Results may differ from a plain program's by a relative error of at most 0.0095.
Values may be sent and summed in bfloat16 or wider, within the bound.
No kernel may reach another device: no remote copies, remote signals or barrier semaphores. Data moves between devices by JAX's collectives and lax.ppermute only.
A program may use at most 64 MiB of HBM per device.

v0:
```python
import jax
import jax.numpy as jnp
from jax import lax
from jax.sharding import PartitionSpec as P


def normalize(tokens, norm_gain):
    widened = tokens.astype(jnp.float32)
    meansq = jnp.mean(widened * widened, axis=-1, keepdims=True)
    return (widened * lax.rsqrt(meansq + 1e-06) * norm_gain).astype(jnp.bfloat16)


def residual_mlp(normed, dense_in, dense_out):
    before_act = jnp.dot(
        normed,
        lax.all_gather(dense_in, "expert", axis=0, tiled=True),
        preferred_element_type=jnp.float32,
    )
    dense_act = jax.nn.gelu(before_act).astype(jnp.bfloat16)
    partial_out = jnp.dot(
        dense_act,
        lax.all_gather(dense_out, "expert", axis=1, tiled=True),
        preferred_element_type=jnp.float32,
    )
    return lax.psum_scatter(
        partial_out.astype(jnp.bfloat16), "cuts", scatter_dimension=1, tiled=True
    ).astype(jnp.float32)


def local(tokens, route, gate_prob, norm_gain, dense_in, dense_out, expert_in, expert_out):
    experts = lax.axis_size("expert")
    slices = lax.axis_size("cuts")
    tok_rows, width = tokens.shape
    share = width // slices
    capacity = max(2, 3 * tok_rows // (2 * experts))
    normed = normalize(tokens, norm_gain)
    dense = residual_mlp(normed, dense_in, dense_out)
    picked = route[:, 0]
    labels = jnp.arange(experts, dtype=jnp.int32)
    one_hot = (picked[:, None] == labels[None, :]).astype(jnp.int32)
    before = jnp.cumsum(one_hot, axis=0) - one_hot
    position = jnp.sum(before * one_hot, axis=-1)
    target = picked * capacity + position
    outgoing = jnp.zeros((experts * capacity, width), jnp.bfloat16).at[target].set(normed)
    outgoing = outgoing.reshape(experts, capacity, width)
    weight_in = expert_in[0]
    weight_out = expert_out[0]
    arrived = lax.all_to_all(outgoing, "expert", split_axis=0, concat_axis=0, tiled=True)
    sources = arrived.shape[0]
    count = arrived.shape[1]
    flat_rows = arrived.reshape(sources * count, width)
    inner = jax.nn.gelu(jnp.dot(flat_rows, weight_in, preferred_element_type=jnp.float32)).astype(
        jnp.bfloat16
    )
    partial_res = jnp.dot(inner, weight_out, preferred_element_type=jnp.float32).reshape(
        sources, count, width
    )
    cut_index = lax.axis_index("cuts")
    own_share = lax.psum_scatter(
        partial_res.astype(jnp.bfloat16), "cuts", scatter_dimension=2, tiled=True
    )
    returned = lax.all_to_all(own_share, "expert", split_axis=0, concat_axis=0, tiled=True)
    expert_res = returned.reshape(experts * capacity, share)[target].astype(jnp.float32)
    own_tokens = lax.dynamic_slice_in_dim(tokens, cut_index * share, share, 1).astype(jnp.float32)
    layer_out = own_tokens + dense + gate_prob[:, None] * expert_res
    return layer_out.astype(jnp.bfloat16)


def solution(mesh):
    return jax.shard_map(
        local,
        mesh=mesh,
        in_specs=(
            P(("groups", "expert"), None),
            P(("groups", "expert"), None),
            P(("groups", "expert")),
            P(),
            P("expert", "cuts"),
            P("cuts", "expert"),
            P("expert", None, "cuts"),
            P("expert", "cuts", None),
        ),
        out_specs=P(("groups", "expert"), "cuts"),
        check_vma=False,
    )
```

profile of v0, /device:TPU:520, one launch (start us, length us, event | category | flops | bytes accessed | tf_op | source)
XLA Modules:
  0.0 242.6 jit_solution(17498431186628819330)
XLA Ops:
  7.4 0.7 all-gather.3.cloned.1.call-update
  8.2 0.1 all-gather.5.cloned.1.call-start
  8.2 0.7 all-gather.5.cloned.1.call-update
  9.0 0.1 reduce-scatter.5.cloned.1.call-start
  9.0 2.1 fusion
  11.1 0.7 fusion.45
  11.8 1.1 reduce-window.6
  13.0 0.2 slice_reduce_fusion
  13.2 0.8 fusion.44
  14.0 0.7 compare_select_fusion
  14.7 5.9 %scatter_custom_fusion = bf16[768,2048]{1,0:T(8,128)(2,1)S(1)} fusion(s32[512]{0:T(512)S(1)} %bitcast.48, bf16[]{:T(256)} %constant.9.clone.1, bf16[512,2048]{1,0:T(8,128)(2,1)} %param.8, f32[2048]{0:T(1024)} %param.11, f32[512]{0:T(512)S(1)} %add_rsqrt_fusion), kind=kCustom, calls=%fused_computation.31 | custom fusion | flops 4194304 | bytes 5253122 | tf_op jit(solution)/shard_map/scatter | solution.py:44
  20.6 107.7 %all_to_all.10 = bf16[16,48,2048]{2,1,0:T(8,128)(2,1)S(1)} all-to-all(bf16[16,48,2048]{2,1,0:T(8,128)(2,1)S(1)} %bitcast.44), channel_id=1, replica_groups=mesh['groups'=2,'expert'=16,'cuts'=8] {'expert'}, dimensions={0} | all-to-all | bytes 6291456 | tf_op jit(solution)/shard_map/all_to_all | solution.py:48
  128.3 4.0 %fusion.17 = bf16[768,1024]{1,0:T(8,128)(2,1)S(1)} fusion(bf16[768,2048]{1,0:T(8,128)(2,1)S(1)} %bitcast.45, bf16[1,2048,1024]{2,1,0:T(8,128)(2,1)S(1)} %copy-done.3), kind=kOutput, calls=%fused_computation.20 | convolution fusion | flops 3228303360 | bytes 8912896 | tf_op jit(solution)/shard_map/dot_general | solution.py:52
  132.2 4.9 %fusion.7 = bf16[16,48,2048]{2,1,0:T(8,128)(2,1)} fusion(bf16[16,48,1024]{2,1,0:T(8,128)(2,1)S(1)} %bitcast.51, bf16[1,1024,2048]{2,1,0:T(8,128)(2,1)S(1)} %copy-done.4), kind=kOutput, calls=%fused_computation.12 | convolution fusion | flops 3222798336 | bytes 8912896 | tf_op jit(solution)/shard_map/dot_general | solution.py:55
  137.1 0.1 reduce-scatter.5.cloned.1.call-update
  137.2 0.2 reduce-scatter.3.cloned.1.call-start
  137.5 26.9 %all-gather.5.cloned.1.call-done = bf16[1024,2048]{1,0:T(8,128)(2,1)} async-done(((bf16[1024,128]{1,0:T(8,128)(2,1)}), bf16[1024,2048]{1,0:T(8,128)(2,1)}) %all-gather.5.cloned.1.call-update) | async-done | bytes 4194320 | tf_op jit(solution)/shard_map/all_gather | solution.py:22
  164.3 9.9 %convolution_convert_fusion = bf16[512,2048]{1,0:T(8,128)(2,1)} fusion(bf16[1024,2048]{1,0:T(8,128)(2,1)} %all-gather.5.cloned.1.call-done, bf16[2048,1024]{1,0:T(8,128)(2,1)} %all-gather.3.cloned.1.call-done, bf16[512,2048]{1,0:T(8,128)(2,1)S(1)} %copy-done, f32[2048]{0:T(1024)S(1)} %copy-done.1, f32[512]{0:T(512)S(1)} %add_rsqrt_fusion), kind=kOutput, calls=%fused_computation.22 | convolution fusion | flops 4304928768 | bytes 12593152 | tf_op jit(solution)/shard_map/dot_general | solution.py:20
  174.3 12.3 %reduce-scatter.5.cloned.1.call-done = bf16[16,48,256]{2,1,0:T(8,128)(2,1)} async-done(((bf16[16,48,2048]{2,1,0:T(8,128)(2,1)}), bf16[16,48,256]{2,1,0:T(8,128)(2,1)}) %reduce-scatter.5.cloned.1.call-update) | async-done | bytes 393232 | tf_op jit(solution)/shard_map/reduce_scatter | solution.py:59
  186.6 7.2 %all-to-all-start.1 = ((bf16[16,48,256]{2,1,0:T(8,128)(2,1)}), bf16[16,48,256]{2,1,0:T(8,128)(2,1)S(1)}, u32[]{:S(2)}, u32[]{:S(2)}) async-start(bf16[16,48,256]{2,1,0:T(8,128)(2,1)} %reduce-scatter.5.cloned.1.call-done), calls=%async_computation.3 | async-start | bytes 786432 | tf_op jit(solution)/shard_map/all_to_all | solution.py:62
  193.9 10.1 %all-to-all-done.1 = bf16[16,48,256]{2,1,0:T(8,128)(2,1)S(1)} async-done(((bf16[16,48,256]{2,1,0:T(8,128)(2,1)}), bf16[16,48,256]{2,1,0:T(8,128)(2,1)S(1)}, u32[]{:S(2)}, u32[]{:S(2)}) %all-to-all-start.1) | async-done | bytes 393248 | tf_op jit(solution)/shard_map/all_to_all | solution.py:62
  204.0 1.9 gather_fusion
  206.0 27.4 %reduce-scatter.3.cloned.1.call-done = bf16[512,256]{1,0:T(8,128)(2,1)} async-done(((bf16[512,2048]{1,0:T(8,128)(2,1)}), bf16[512,256]{1,0:T(8,128)(2,1)}) %reduce-scatter.3.cloned.1.call-update) | async-done | bytes 262160 | tf_op jit(solution)/shard_map/reduce_scatter | solution.py:25
  233.4 1.8 add_convert_fusion
  (17 shorter events, 0.2 us)
Async XLA Ops:
  7.4 130.0 %all-gather.3.cloned.1.call-start = ((), (), s32[]{:S(2)}) async-start(), calls=%async_computation.4 | async-start | bytes 4456448 | tf_op jit(solution)/shard_map/all_gather | solution.py:16
  8.2 156.2 %all-gather.5.cloned.1.call-start = ((), (), s32[]{:S(2)}) async-start(), calls=%async_computation.5 | async-start | bytes 4456448 | tf_op jit(solution)/shard_map/all_gather | solution.py:22
  9.0 177.6 %reduce-scatter.5.cloned.1.call-start = ((), (), s32[]{:S(2)}) async-start(), calls=%async_computation.7 | async-start | bytes 3538944 | tf_op jit(solution)/shard_map/reduce_scatter | solution.py:59
  20.5 107.7 %copy-start.3 = (bf16[1,2048,1024]{2,1,0:T(8,128)(2,1)S(1)}, bf16[1,2048,1024]{2,1,0:T(8,128)(2,1)}, u32[]{:S(2)}) copy-start(bf16[1,2048,1024]{2,1,0:T(8,128)(2,1)} %param.14) | copy-start | bytes 12582916
  128.3 4.0 %copy-start.4 = (bf16[1,1024,2048]{2,1,0:T(8,128)(2,1)S(1)}, bf16[1,1024,2048]{2,1,0:T(8,128)(2,1)}, u32[]{:S(2)}) copy-start(bf16[1,1024,2048]{2,1,0:T(8,128)(2,1)} %param.15) | copy-start | bytes 12582916
  137.1 27.2 %copy-start = (bf16[512,2048]{1,0:T(8,128)(2,1)S(1)}, bf16[512,2048]{1,0:T(8,128)(2,1)}, u32[]{:S(2)}) copy-start(bf16[512,2048]{1,0:T(8,128)(2,1)} %param.8) | copy-start | bytes 6291460
  137.1 27.2 %copy-start.1 = (f32[2048]{0:T(1024)S(1)}, f32[2048]{0:T(1024)}, u32[]{:S(2)}) copy-start(f32[2048]{0:T(1024)} %param.11) | copy-start | bytes 24580
  137.2 96.2 %reduce-scatter.3.cloned.1.call-start = ((), (), s32[]{:S(2)}) async-start(), calls=%async_computation.6 | async-start | bytes 2359296 | tf_op jit(solution)/shard_map/reduce_scatter | solution.py:25
  174.2 59.1 %copy-start.2 = (f32[512]{0:T(512)S(1)}, f32[512]{0:T(512)}, u32[]{:S(2)}) copy-start(f32[512]{0:T(512)} %param.10) | copy-start | bytes 6148
  186.6 17.4 %all-to-all-start.1 = ((bf16[16,48,256]{2,1,0:T(8,128)(2,1)}), bf16[16,48,256]{2,1,0:T(8,128)(2,1)S(1)}, u32[]{:S(2)}, u32[]{:S(2)}) async-start(bf16[16,48,256]{2,1,0:T(8,128)(2,1)} %reduce-scatter.5.cloned.1.call-done), calls=%async_computation.3 | async-start | bytes 786432 | tf_op jit(solution)/shard_map/all_to_all | solution.py:62
Sparse Core Ops, SparseCore 0:
  10.0 97.4 all-gather.2
  109.3 55.0 all-gather.4
Sparse Core Ops, SparseCore 1:
  137.3 49.3 reduce-scatter.4
  189.1 44.2 reduce-scatter.2
where the time goes:
time: 243 us
  blocking collectives  108 us (44%)
  waiting for transfers between devices  78.3 us (32%)
  matrix products  18.7 us (8%)
  between operations  15 us (6%)
  other arithmetic  13.1 us (5%)
  starting transfers between devices  7.62 us (3%)
    all_to_all x1, blocking collectives, local(): lax.all_to_all(outgoing, 'expert', split_axis=0, concat_axis=0, tiled=True)  108 us
    reduce_scatter x1, waiting for transfers between devices, residual_mlp(): lax.psum_scatter(partial_out.astype(jnp.bfloat16), 'cuts', scatter_dimens...  27.4 us
    all_gather x1, waiting for transfers between devices, residual_mlp(): lax.all_gather(dense_out, 'expert', axis=1, tiled=True)  26.9 us
    reduce_scatter x1, waiting for transfers between devices, local(): lax.psum_scatter(partial_res.astype(jnp.bfloat16), 'cuts', scatter_dimens...  12.3 us
    all_to_all x1, waiting for transfers between devices, local(): lax.all_to_all(own_share, 'expert', split_axis=0, concat_axis=0, tiled=True)  10.1 us
    dot_general x1, matrix products, residual_mlp(): jnp.dot(dense_act, lax.all_gather(dense_out, 'expert', axis=1, tiled=True...  9.9 us
    all_to_all x1, starting transfers between devices, local(): lax.all_to_all(own_share, 'expert', split_axis=0, concat_axis=0, tiled=True)  7.24 us
    scatter x1, other arithmetic, local(): jnp.zeros((experts * capacity, width), jnp.bfloat16).at[target].set(normed)  5.85 us
  transfers between devices with their start and end apart: 5, of which 4 were waited for; matrix products, arithmetic and copies ran while one was open for 13% of the time, Pallas kernels for 0%

commit v1 on v0

v1 whole, which is shorter than its diff:
```python
import jax
import jax.numpy as jnp
from jax import lax
from jax.sharding import PartitionSpec as P


def matmul(lhs, rhs):
    return jnp.dot(lhs, rhs, preferred_element_type=jnp.float32)


def wrapped(index, size):
    return jnp.where(index < 0, index + size, jnp.where(index < size, index, index - size))


def turn(values, axis, step):
    size = lax.axis_size(axis)
    return lax.ppermute(values, axis, [(i, (i + step) % size) for i in range(size)])


def ring_gather_product(own, weight, axis):
    size = lax.axis_size(axis)
    rank = lax.axis_index(axis)
    rows = own.shape[1]

    def rows_of(offset):
        return lax.dynamic_slice_in_dim(weight, wrapped(rank + offset, size) * rows, rows, 0)

    ahead = back = own
    total = matmul(own, rows_of(0))
    for hop in range(1, size // 2 + 1):
        ahead = turn(ahead, axis, 1)
        if hop <= (size - 1) // 2:
            back = turn(back, axis, -1)
            total = total + matmul(ahead, rows_of(-hop)) + matmul(back, rows_of(hop))
        else:
            total = total + matmul(ahead, rows_of(-hop))
    return total


def ring_scatter(partial_for, axis):
    size = lax.axis_size(axis)

    def chain(hops, step):
        carried = partial_for(step * hops).astype(jnp.bfloat16)
        for left in range(hops - 1, -1, -1):
            carried = turn(carried, axis, step)
            if left:
                carried = (carried.astype(jnp.float32) + partial_for(step * left)).astype(jnp.bfloat16)
        return carried.astype(jnp.float32)

    return partial_for(0) + chain(size // 2, 1) + chain((size - 1) // 2, -1)


def local(tokens, route, gate_prob, norm_gain, dense_in, dense_out, expert_in, expert_out):
    experts = lax.axis_size("expert")
    slices = lax.axis_size("cuts")
    cut = lax.axis_index("cuts")
    tok_rows, width = tokens.shape
    share = width // slices
    capacity = max(2, 3 * tok_rows // (2 * experts))
    slots = experts * capacity

    def columns(array, offset):
        return lax.dynamic_slice_in_dim(array, wrapped(cut + offset, slices) * share, share, array.ndim - 1)

    hidden = dense_in.shape[1]
    both = lax.all_gather(jnp.concatenate([dense_in, dense_out.T], axis=1), "expert", axis=0, tiled=True)
    full_in, full_out = both[:, :hidden], both[:, hidden:].T

    widened = tokens.astype(jnp.float32)
    scale = lax.rsqrt(jnp.mean(widened * widened, axis=-1, keepdims=True) + 1e-06)
    own_tokens = columns(tokens, 0).astype(jnp.float32)
    own_normed = (own_tokens * scale * columns(norm_gain, 0)).astype(jnp.bfloat16)

    picked = route[:, 0]
    one_hot = picked[:, None] == jnp.arange(experts, dtype=jnp.int32)[None, :]
    order = jnp.arange(tok_rows, dtype=jnp.int32)
    earlier = (order[None, :] < order[:, None]).astype(jnp.bfloat16)
    before = matmul(earlier, one_hot.astype(jnp.bfloat16))
    position = jnp.sum(jnp.where(one_hot, before, 0.0), axis=-1).astype(jnp.int32)
    target = picked * capacity + position
    slot_ids = jnp.arange(slots, dtype=jnp.int32)
    to_slots = (slot_ids[:, None] == target[None, :]).astype(jnp.bfloat16)
    from_slots = (target[:, None] == slot_ids[None, :]).astype(jnp.bfloat16)

    outgoing = matmul(to_slots, own_normed).astype(jnp.bfloat16)
    arrived = lax.all_to_all(
        outgoing.reshape(experts, capacity, share), "expert", split_axis=0, concat_axis=0, tiled=True
    ).reshape(slots, share)
    inner = jax.nn.gelu(ring_gather_product(arrived, expert_in[0], "cuts")).astype(jnp.bfloat16)
    weight_out = expert_out[0]
    own_share = ring_scatter(lambda offset: matmul(inner, columns(weight_out, offset)), "cuts").astype(jnp.bfloat16)
    returned = lax.all_to_all(
        own_share.reshape(experts, capacity, share), "expert", split_axis=0, concat_axis=0, tiled=True
    ).reshape(slots, share)
    expert_res = matmul(from_slots, returned)

    normed = (widened * scale * norm_gain).astype(jnp.bfloat16)
    dense_act = jax.nn.gelu(matmul(normed, full_in)).astype(jnp.bfloat16)
    dense = ring_scatter(lambda offset: matmul(dense_act, columns(full_out, offset)), "cuts")

    return (own_tokens + dense + gate_prob[:, None] * expert_res).astype(jnp.bfloat16)


def solution(mesh):
    return jax.shard_map(
        local,
        mesh=mesh,
        in_specs=(
            P(("groups", "expert"), None),
            P(("groups", "expert"), None),
            P(("groups", "expert")),
            P(),
            P("expert", "cuts"),
            P("cuts", "expert"),
            P("expert", None, "cuts"),
            P("expert", "cuts", None),
        ),
        out_specs=P(("groups", "expert"), "cuts"),
        check_vma=False,
    )
```

time: 243 us -> 197 us (0.81)
  blocking collectives: 108 us -> 33.2 us
  starting transfers between devices: 7.62 us -> 35.9 us
  other arithmetic: 13.1 us -> 3.66 us
  matrix products: 18.7 us -> 27.8 us
    ppermute x0 -> x21, waiting for transfers between devices: none -> 79.3 us  [turn(): lax.ppermute(values, axis, [(i, (i + step) % size) for i in range(size)])]
    all_to_all x1, blocking collectives: 108 us -> 33.2 us  [local(): lax.all_to_all(outgoing.reshape(experts, capacity, share), 'expert', spli...]
    reduce_scatter x2 -> x0, waiting for transfers between devices: 39.7 us -> none  [the longest x1 27.4 us: residual_mlp(): lax.psum_scatter(partial_out.astype(jnp.bfloat16), 'cuts', scatter_dimens...]
    ppermute x0 -> x21, starting transfers between devices: none -> 28.2 us  [turn(): lax.ppermute(values, axis, [(i, (i + step) % size) for i in range(size)])]
    all_gather x2 -> x1, waiting for transfers between devices: 26.9 us -> 0.01 us  [local(): lax.all_gather(jnp.concatenate([dense_in, dense_out.T], axis=1), 'expert'...]
    all_to_all x1, waiting for transfers between devices: 10.1 us -> 0.01 us  [local(): lax.all_to_all(own_share.reshape(experts, capacity, share), 'expert', spl...]
    dot_general x3 -> x28, matrix products: 18.7 us -> 27.8 us  [matmul(): return jnp.dot(lhs, rhs, preferred_element_type=jnp.float32)]
    scatter x1 -> x0, other arithmetic: 5.85 us -> none  [local(): jnp.zeros((experts * capacity, width), jnp.bfloat16).at[target].set(normed)]
  transfers between devices with their start and end apart: 5 -> 23, of which waited for: 4 -> 13; matrix products, arithmetic and copies ran while one was open for 13% -> 15% of each run, Pallas kernels for 0% -> 0%
where the time goes in v1:
time: 197 us; the launch traced here: 196 us
  waiting for transfers between devices  79.4 us (40%)
  starting transfers between devices  35.9 us (18%)
  blocking collectives  33.2 us (17%)
  matrix products  27.8 us (14%)
  between operations  13.9 us (7%)
  other arithmetic  3.66 us (2%)
  local copies, waits for them, and re-layouts  2.65 us (1%)
    ppermute x21, waiting for transfers between devices, turn(): lax.ppermute(values, axis, [(i, (i + step) % size) for i in range(size)])  79.3 us
    all_to_all x1, blocking collectives, local(): lax.all_to_all(outgoing.reshape(experts, capacity, share), 'expert', spli...  33.2 us
    ppermute x21, starting transfers between devices, turn(): lax.ppermute(values, axis, [(i, (i + step) % size) for i in range(size)])  28.2 us
    dot_general x28, matrix products, matmul(): return jnp.dot(lhs, rhs, preferred_element_type=jnp.float32)  27.8 us
    all_to_all x1, starting transfers between devices, local(): lax.all_to_all(own_share.reshape(experts, capacity, share), 'expert', spl...  7.68 us
  transfers between devices with their start and end apart: 23, of which 13 were waited for; matrix products, arithmetic and copies ran while one was open for 15% of the time, Pallas kernels for 0%

profile of v1, /device:TPU:520, one launch (start us, length us, event | category | flops | bytes accessed | tf_op | source)
XLA Modules:
  0.0 196.5 jit_solution(196233090280595289)
XLA Ops:
  12.6 33.2 %all_to_all.10 = bf16[16,48,256]{2,1,0:T(8,128)(2,1)S(1)} all-to-all(bf16[16,48,256]{2,1,0:T(8,128)(2,1)S(1)} %bitcast.89), channel_id=1, replica_groups=mesh['groups'=2,'expert'=16,'cuts'=8] {'expert'}, dimensions={0} | all-to-all | bytes 786432 | tf_op jit(solution)/shard_map/all_to_all | solution.py:87
  45.8 2.0 %collective-permute-start.7 = (bf16[768,256]{1,0:T(8,128)(2,1)S(1)}, bf16[768,256]{1,0:T(8,128)(2,1)S(1)}, u32[]{:S(2)}, u32[]{:S(2)}) collective-permute-start(bf16[768,256]{1,0:T(8,128)(2,1)S(1)} %bitcast.86), channel_id=1, source_target_pairs={{0,1},{1,2},{2,3},{3,4},{4,5},{5,6},{6,7},{7,0},{8,9},{9,10},{10,1... | collective-permute-start | bytes 1179656 | tf_op jit(solution)/shard_map/ppermute | solution.py:17
  49.6 8.0 %collective-permute-done.8 = bf16[768,256]{1,0:T(8,128)(2,1)S(1)} collective-permute-done((bf16[768,256]{1,0:T(8,128)(2,1)S(1)}, bf16[768,256]{1,0:T(8,128)(2,1)S(1)}, u32[]{:S(2)}, u32[]{:S(2)}) %collective-permute-start.8) | collective-permute-done | bytes 393248 | tf_op jit(solution)/shard_map/ppermute | solution.py:17
  61.8 6.8 %collective-permute-done.10 = bf16[768,256]{1,0:T(8,128)(2,1)S(1)} collective-permute-done((bf16[768,256]{1,0:T(8,128)(2,1)S(1)}, bf16[768,256]{1,0:T(8,128)(2,1)S(1)}, u32[]{:S(2)}, u32[]{:S(2)}) %collective-permute-start.10) | collective-permute-done | bytes 393248 | tf_op jit(solution)/shard_map/ppermute | solution.py:17
  68.6 2.7 %collective-permute-start.12 = (bf16[768,256]{1,0:T(8,128)(2,1)S(1)}, bf16[768,256]{1,0:T(8,128)(2,1)S(1)}, u32[]{:S(2)}, u32[]{:S(2)}) collective-permute-start(bf16[768,256]{1,0:T(8,128)(2,1)S(1)} %collective-permute-done.10), channel_id=1, source_target_pairs={{0,7},{1,0},{2,1},{3,2},{4,3},{5,4},{6,5},{7,6},{8,15},{9,8},{10,9... | collective-permute-start | bytes 1179656 | tf_op jit(solution)/shard_map/ppermute | solution.py:17
  72.5 10.0 %collective-permute-done.11 = bf16[768,256]{1,0:T(8,128)(2,1)S(1)} collective-permute-done((bf16[768,256]{1,0:T(8,128)(2,1)S(1)}, bf16[768,256]{1,0:T(8,128)(2,1)S(1)}, u32[]{:S(2)}, u32[]{:S(2)}) %collective-permute-start.11) | collective-permute-done | bytes 393248 | tf_op jit(solution)/shard_map/ppermute | solution.py:17
  83.7 9.2 %collective-permute-done.13 = bf16[768,256]{1,0:T(8,128)(2,1)S(1)} collective-permute-done((bf16[768,256]{1,0:T(8,128)(2,1)S(1)}, bf16[768,256]{1,0:T(8,128)(2,1)S(1)}, u32[]{:S(2)}, u32[]{:S(2)}) %collective-permute-start.13) | collective-permute-done | bytes 393248 | tf_op jit(solution)/shard_map/ppermute | solution.py:17
  98.4 3.3 %collective-permute-start.18 = (bf16[768,256]{1,0:T(8,128)(2,1)S(1)}, bf16[768,256]{1,0:T(8,128)(2,1)S(1)}, u32[]{:S(2)}, u32[]{:S(2)}) collective-permute-start(bf16[768,256]{1,0:T(8,128)(2,1)S(1)} %convolution_convert_fusion), channel_id=1, source_target_pairs={{0,7},{1,0},{2,1},{3,2},{4,3},{5,4},{6,5},{7,6},{8,15},{9,8},{10,9... | collective-permute-start | bytes 1179656 | tf_op jit(solution)/shard_map/ppermute | solution.py:17
  102.3 4.0 %collective-permute-done.14 = bf16[768,256]{1,0:T(8,128)(2,1)S(1)} collective-permute-done((bf16[768,256]{1,0:T(8,128)(2,1)S(1)}, bf16[768,256]{1,0:T(8,128)(2,1)S(1)}, u32[]{:S(2)}, u32[]{:S(2)}) %collective-permute-start.14) | collective-permute-done | bytes 393248 | tf_op jit(solution)/shard_map/ppermute | solution.py:17
  108.4 3.4 %collective-permute-start.19 = (bf16[768,256]{1,0:T(8,128)(2,1)S(1)}, bf16[768,256]{1,0:T(8,128)(2,1)S(1)}, u32[]{:S(2)}, u32[]{:S(2)}) collective-permute-start(bf16[768,256]{1,0:T(8,128)(2,1)S(1)} %add_convert_fusion.2), channel_id=1, source_target_pairs={{0,7},{1,0},{2,1},{3,2},{4,3},{5,4},{6,5},{7,6},{8,15},{9,8},{10,9... | collective-permute-start | bytes 1179656 | tf_op jit(solution)/shard_map/ppermute | solution.py:17
  111.8 4.9 %collective-permute-done.15 = bf16[768,256]{1,0:T(8,128)(2,1)S(1)} collective-permute-done((bf16[768,256]{1,0:T(8,128)(2,1)S(1)}, bf16[768,256]{1,0:T(8,128)(2,1)S(1)}, u32[]{:S(2)}, u32[]{:S(2)}) %collective-permute-start.15) | collective-permute-done | bytes 393248 | tf_op jit(solution)/shard_map/ppermute | solution.py:17
  118.1 3.8 %collective-permute-start.20 = (bf16[768,256]{1,0:T(8,128)(2,1)S(1)}, bf16[768,256]{1,0:T(8,128)(2,1)S(1)}, u32[]{:S(2)}, u32[]{:S(2)}) collective-permute-start(bf16[768,256]{1,0:T(8,128)(2,1)S(1)} %add_convert_fusion.1), channel_id=1, source_target_pairs={{0,7},{1,0},{2,1},{3,2},{4,3},{5,4},{6,5},{7,6},{8,15},{9,8},{10,9... | collective-permute-start | bytes 1179656 | tf_op jit(solution)/shard_map/ppermute | solution.py:17
  121.9 5.8 %collective-permute-done.16 = bf16[768,256]{1,0:T(8,128)(2,1)S(1)} collective-permute-done((bf16[768,256]{1,0:T(8,128)(2,1)S(1)}, bf16[768,256]{1,0:T(8,128)(2,1)S(1)}, u32[]{:S(2)}, u32[]{:S(2)}) %collective-permute-start.16) | collective-permute-done | bytes 393248 | tf_op jit(solution)/shard_map/ppermute | solution.py:17
  128.5 8.3 %collective-permute-done.17 = bf16[768,256]{1,0:T(8,128)(2,1)S(1)} collective-permute-done((bf16[768,256]{1,0:T(8,128)(2,1)S(1)}, bf16[768,256]{1,0:T(8,128)(2,1)S(1)}, u32[]{:S(2)}, u32[]{:S(2)}) %collective-permute-start.17) | collective-permute-done | bytes 393248 | tf_op jit(solution)/shard_map/ppermute | solution.py:17
  137.7 7.7 %all-to-all-start.1 = ((bf16[16,48,256]{2,1,0:T(8,128)(2,1)}), bf16[16,48,256]{2,1,0:T(8,128)(2,1)S(1)}, u32[]{:S(2)}, u32[]{:S(2)}) async-start(bf16[16,48,256]{2,1,0:T(8,128)(2,1)} %bitcast.22), calls=%async_computation.1 | async-start | bytes 786432 | tf_op jit(solution)/shard_map/all_to_all | solution.py:93
  145.5 5.1 %fusion.20 = bf16[512,1024]{1,0:T(8,128)(2,1)S(1)} fusion(bf16[2048,2048]{0,1:T(8,128)(2,1)} %all-gather.2.cloned.1.call-done, bf16[512,2048]{1,0:T(8,128)(2,1)S(1)} %copy-done.2, f32[2048]{0:T(1024)S(1)} %copy-done.6, f32[512]{0:T(512)S(1)} %add_rsqrt_fusion), kind=kOutput, calls=%fused_computation.24 | convolution fusion | flops 2156396544 | bytes 7350272 | tf_op jit(solution)/shard_map/dot_general | solution.py:8
  152.7 3.2 %collective-permute-start.4 = (bf16[512,256]{1,0:T(8,128)(2,1)S(1)}, bf16[512,256]{1,0:T(8,128)(2,1)S(1)}, u32[]{:S(2)}, u32[]{:S(2)}) collective-permute-start(bf16[512,256]{1,0:T(8,128)(2,1)S(1)} %convolution_convert_fusion.2), channel_id=1, source_target_pairs={{0,7},{1,0},{2,1},{3,2},{4,3},{5,4},{6,5},{7,6},{8,15},{9,8},{10,9... | collective-permute-start | bytes 786440 | tf_op jit(solution)/shard_map/ppermute | solution.py:17
  156.4 5.9 %collective-permute-done = bf16[512,256]{1,0:T(8,128)(2,1)S(1)} collective-permute-done((bf16[512,256]{1,0:T(8,128)(2,1)S(1)}, bf16[512,256]{1,0:T(8,128)(2,1)S(1)}, u32[]{:S(2)}, u32[]{:S(2)}) %collective-permute-start) | collective-permute-done | bytes 262176 | tf_op jit(solution)/shard_map/ppermute | solution.py:17
  163.3 3.3 %collective-permute-start.5 = (bf16[512,256]{1,0:T(8,128)(2,1)S(1)}, bf16[512,256]{1,0:T(8,128)(2,1)S(1)}, u32[]{:S(2)}, u32[]{:S(2)}) collective-permute-start(bf16[512,256]{1,0:T(8,128)(2,1)S(1)} %add_convert_fusion.7), channel_id=1, source_target_pairs={{0,7},{1,0},{2,1},{3,2},{4,3},{5,4},{6,5},{7,6},{8,15},{9,8},{10,9... | collective-permute-start | bytes 786440 | tf_op jit(solution)/shard_map/ppermute | solution.py:17
  166.6 4.9 %collective-permute-done.1 = bf16[512,256]{1,0:T(8,128)(2,1)S(1)} collective-permute-done((bf16[512,256]{1,0:T(8,128)(2,1)S(1)}, bf16[512,256]{1,0:T(8,128)(2,1)S(1)}, u32[]{:S(2)}, u32[]{:S(2)}) %collective-permute-start.1) | collective-permute-done | bytes 262176 | tf_op jit(solution)/shard_map/ppermute | solution.py:17
  172.3 3.3 %collective-permute-start.6 = (bf16[512,256]{1,0:T(8,128)(2,1)S(1)}, bf16[512,256]{1,0:T(8,128)(2,1)}, u32[]{:S(2)}, u32[]{:S(2)}) collective-permute-start(bf16[512,256]{1,0:T(8,128)(2,1)S(1)} %add_convert_fusion.6), channel_id=1, source_target_pairs={{0,7},{1,0},{2,1},{3,2},{4,3},{5,4},{6,5},{7,6},{8,15},{9,8},{10,9... | collective-permute-start | bytes 786440 | tf_op jit(solution)/shard_map/ppermute | solution.py:17
  175.6 3.9 %collective-permute-done.2 = bf16[512,256]{1,0:T(8,128)(2,1)S(1)} collective-permute-done((bf16[512,256]{1,0:T(8,128)(2,1)S(1)}, bf16[512,256]{1,0:T(8,128)(2,1)S(1)}, u32[]{:S(2)}, u32[]{:S(2)}) %collective-permute-start.2) | collective-permute-done | bytes 262176 | tf_op jit(solution)/shard_map/ppermute | solution.py:17
  180.2 7.2 %collective-permute-done.3 = bf16[512,256]{1,0:T(8,128)(2,1)} collective-permute-done((bf16[512,256]{1,0:T(8,128)(2,1)S(1)}, bf16[512,256]{1,0:T(8,128)(2,1)}, u32[]{:S(2)}, u32[]{:S(2)}) %collective-permute-start.3) | collective-permute-done | bytes 262176 | tf_op jit(solution)/shard_map/ppermute | solution.py:17
  187.4 2.2 %fusion.36 = bf16[512,256]{1,0:T(8,128)(2,1)} fusion(bf16[512,256]{1,0:T(8,128)(2,1)} %collective-permute-done.6, f32[512,256]{1,0:T(8,128)S(1)} %fusion.100, bf16[512,256]{1,0:T(8,128)(2,1)} %collective-permute-done.3, bf16[768,256]{1,0:T(8,128)(2,1)S(1)} %bitcast.88, s32[512]{0:T(512)S(1)} %bitcast.94, f32[512]{0:T(512)S(1)} %copy-done.7, ...), kind=kOutput, calls=%fused_computation.51 | convolution fusion | flops 202899456 | bytes 1970180 | tf_op jit(solution)/shard_map/dot_general | solution.py:8
  (84 shorter events, 30.4 us)
Async XLA Ops:
  6.6 138.9 %all-gather.2.cloned.1.call-start = ((), (), s32[]{:S(2)}) async-start(), calls=%async_computation.2 | async-start | bytes 8912896 | tf_op jit(solution)/shard_map/all_gather | solution.py:67
  45.8 11.8 %collective-permute-start.8 = (bf16[768,256]{1,0:T(8,128)(2,1)S(1)}, bf16[768,256]{1,0:T(8,128)(2,1)S(1)}, u32[]{:S(2)}, u32[]{:S(2)}) collective-permute-start(bf16[768,256]{1,0:T(8,128)(2,1)S(1)} %bitcast.85), channel_id=1, source_target_pairs={{0,7},{1,0},{2,1},{3,2},{4,3},{5,4},{6,5},{7,6},{8,15},{9,8},{10,9... | collective-permute-start | bytes 1179656 | tf_op jit(solution)/shard_map/ppermute | solution.py:17
  45.8 13.1 %collective-permute-start.7 = (bf16[768,256]{1,0:T(8,128)(2,1)S(1)}, bf16[768,256]{1,0:T(8,128)(2,1)S(1)}, u32[]{:S(2)}, u32[]{:S(2)}) collective-permute-start(bf16[768,256]{1,0:T(8,128)(2,1)S(1)} %bitcast.86), channel_id=1, source_target_pairs={{0,1},{1,2},{2,3},{3,4},{4,5},{5,6},{6,7},{7,0},{8,9},{9,10},{10,1... | collective-permute-start | bytes 1179656 | tf_op jit(solution)/shard_map/ppermute | solution.py:17
  57.6 11.0 %collective-permute-start.10 = (bf16[768,256]{1,0:T(8,128)(2,1)S(1)}, bf16[768,256]{1,0:T(8,128)(2,1)S(1)}, u32[]{:S(2)}, u32[]{:S(2)}) collective-permute-start(bf16[768,256]{1,0:T(8,128)(2,1)S(1)} %collective-permute-done.8), channel_id=1, source_target_pairs={{0,7},{1,0},{2,1},{3,2},{4,3},{5,4},{6,5},{7,6},{8,15},{9,8},{10,9... | collective-permute-start | bytes 1179656 | tf_op jit(solution)/shard_map/ppermute | solution.py:17
  59.0 12.3 %collective-permute-start.9 = (bf16[768,256]{1,0:T(8,128)(2,1)S(1)}, bf16[768,256]{1,0:T(8,128)(2,1)S(1)}, u32[]{:S(2)}, u32[]{:S(2)}) collective-permute-start(bf16[768,256]{1,0:T(8,128)(2,1)S(1)} %collective-permute-done.7), channel_id=1, source_target_pairs={{0,1},{1,2},{2,3},{3,4},{4,5},{5,6},{6,7},{7,0},{8,9},{9,10},{10,1... | collective-permute-start | bytes 1179656 | tf_op jit(solution)/shard_map/ppermute | solution.py:17
  68.6 14.5 %collective-permute-start.12 = (bf16[768,256]{1,0:T(8,128)(2,1)S(1)}, bf16[768,256]{1,0:T(8,128)(2,1)S(1)}, u32[]{:S(2)}, u32[]{:S(2)}) collective-permute-start(bf16[768,256]{1,0:T(8,128)(2,1)S(1)} %collective-permute-done.10), channel_id=1, source_target_pairs={{0,7},{1,0},{2,1},{3,2},{4,3},{5,4},{6,5},{7,6},{8,15},{9,8},{10,9... | collective-permute-start | bytes 1179656 | tf_op jit(solution)/shard_map/ppermute | solution.py:17
  71.3 11.2 %collective-permute-start.11 = (bf16[768,256]{1,0:T(8,128)(2,1)S(1)}, bf16[768,256]{1,0:T(8,128)(2,1)S(1)}, u32[]{:S(2)}, u32[]{:S(2)}) collective-permute-start(bf16[768,256]{1,0:T(8,128)(2,1)S(1)} %collective-permute-done.9), channel_id=1, source_target_pairs={{0,1},{1,2},{2,3},{3,4},{4,5},{5,6},{6,7},{7,0},{8,9},{9,10},{10,1... | collective-permute-start | bytes 1179656 | tf_op jit(solution)/shard_map/ppermute | solution.py:17
  82.5 10.4 %collective-permute-start.13 = (bf16[768,256]{1,0:T(8,128)(2,1)S(1)}, bf16[768,256]{1,0:T(8,128)(2,1)S(1)}, u32[]{:S(2)}, u32[]{:S(2)}) collective-permute-start(bf16[768,256]{1,0:T(8,128)(2,1)S(1)} %collective-permute-done.11), channel_id=1, source_target_pairs={{0,1},{1,2},{2,3},{3,4},{4,5},{5,6},{6,7},{7,0},{8,9},{9,10},{10,1... | collective-permute-start | bytes 1179656 | tf_op jit(solution)/shard_map/ppermute | solution.py:17
  96.7 9.7 %collective-permute-start.14 = (bf16[768,256]{1,0:T(8,128)(2,1)S(1)}, bf16[768,256]{1,0:T(8,128)(2,1)S(1)}, u32[]{:S(2)}, u32[]{:S(2)}) collective-permute-start(bf16[768,256]{1,0:T(8,128)(2,1)S(1)} %convolution_convert_fusion.1), channel_id=1, source_target_pairs={{0,1},{1,2},{2,3},{3,4},{4,5},{5,6},{6,7},{7,0},{8,9},{9,10},{10,1... | collective-permute-start | bytes 1179656 | tf_op jit(solution)/shard_map/ppermute | solution.py:17
  98.4 9.3 %collective-permute-start.18 = (bf16[768,256]{1,0:T(8,128)(2,1)S(1)}, bf16[768,256]{1,0:T(8,128)(2,1)S(1)}, u32[]{:S(2)}, u32[]{:S(2)}) collective-permute-start(bf16[768,256]{1,0:T(8,128)(2,1)S(1)} %convolution_convert_fusion), channel_id=1, source_target_pairs={{0,7},{1,0},{2,1},{3,2},{4,3},{5,4},{6,5},{7,6},{8,15},{9,8},{10,9... | collective-permute-start | bytes 1179656 | tf_op jit(solution)/shard_map/ppermute | solution.py:17
  107.0 9.7 %collective-permute-start.15 = (bf16[768,256]{1,0:T(8,128)(2,1)S(1)}, bf16[768,256]{1,0:T(8,128)(2,1)S(1)}, u32[]{:S(2)}, u32[]{:S(2)}) collective-permute-start(bf16[768,256]{1,0:T(8,128)(2,1)S(1)} %add_convert_fusion.5), channel_id=1, source_target_pairs={{0,1},{1,2},{2,3},{3,4},{4,5},{5,6},{6,7},{7,0},{8,9},{9,10},{10,1... | collective-permute-start | bytes 1179656 | tf_op jit(solution)/shard_map/ppermute | solution.py:17
  108.4 9.6 %collective-permute-start.19 = (bf16[768,256]{1,0:T(8,128)(2,1)S(1)}, bf16[768,256]{1,0:T(8,128)(2,1)S(1)}, u32[]{:S(2)}, u32[]{:S(2)}) collective-permute-start(bf16[768,256]{1,0:T(8,128)(2,1)S(1)} %add_convert_fusion.2), channel_id=1, source_target_pairs={{0,7},{1,0},{2,1},{3,2},{4,3},{5,4},{6,5},{7,6},{8,15},{9,8},{10,9... | collective-permute-start | bytes 1179656 | tf_op jit(solution)/shard_map/ppermute | solution.py:17
  116.8 10.8 %collective-permute-start.16 = (bf16[768,256]{1,0:T(8,128)(2,1)S(1)}, bf16[768,256]{1,0:T(8,128)(2,1)S(1)}, u32[]{:S(2)}, u32[]{:S(2)}) collective-permute-start(bf16[768,256]{1,0:T(8,128)(2,1)S(1)} %add_convert_fusion.4), channel_id=1, source_target_pairs={{0,1},{1,2},{2,3},{3,4},{4,5},{5,6},{6,7},{7,0},{8,9},{9,10},{10,1... | collective-permute-start | bytes 1179656 | tf_op jit(solution)/shard_map/ppermute | solution.py:17
  118.1 10.4 %collective-permute-start.20 = (bf16[768,256]{1,0:T(8,128)(2,1)S(1)}, bf16[768,256]{1,0:T(8,128)(2,1)S(1)}, u32[]{:S(2)}, u32[]{:S(2)}) collective-permute-start(bf16[768,256]{1,0:T(8,128)(2,1)S(1)} %add_convert_fusion.1), channel_id=1, source_target_pairs={{0,7},{1,0},{2,1},{3,2},{4,3},{5,4},{6,5},{7,6},{8,15},{9,8},{10,9... | collective-permute-start | bytes 1179656 | tf_op jit(solution)/shard_map/ppermute | solution.py:17
  127.7 17.7 %copy-start.2 = (bf16[512,2048]{1,0:T(8,128)(2,1)S(1)}, bf16[512,2048]{1,0:T(8,128)(2,1)}, u32[]{:S(2)}) copy-start(bf16[512,2048]{1,0:T(8,128)(2,1)} %param.8) | copy-start | bytes 6291460
  127.8 9.1 %collective-permute-start.17 = (bf16[768,256]{1,0:T(8,128)(2,1)S(1)}, bf16[768,256]{1,0:T(8,128)(2,1)S(1)}, u32[]{:S(2)}, u32[]{:S(2)}) collective-permute-start(bf16[768,256]{1,0:T(8,128)(2,1)S(1)} %add_convert_fusion.3), channel_id=1, source_target_pairs={{0,1},{1,2},{2,3},{3,4},{4,5},{5,6},{6,7},{7,0},{8,9},{9,10},{10,1... | collective-permute-start | bytes 1179656 | tf_op jit(solution)/shard_map/ppermute | solution.py:17
  137.7 42.5 %all-to-all-start.1 = ((bf16[16,48,256]{2,1,0:T(8,128)(2,1)}), bf16[16,48,256]{2,1,0:T(8,128)(2,1)S(1)}, u32[]{:S(2)}, u32[]{:S(2)}) async-start(bf16[16,48,256]{2,1,0:T(8,128)(2,1)} %bitcast.22), calls=%async_computation.1 | async-start | bytes 786432 | tf_op jit(solution)/shard_map/all_to_all | solution.py:93
  152.6 9.7 %collective-permute-start = (bf16[512,256]{1,0:T(8,128)(2,1)S(1)}, bf16[512,256]{1,0:T(8,128)(2,1)S(1)}, u32[]{:S(2)}, u32[]{:S(2)}) collective-permute-start(bf16[512,256]{1,0:T(8,128)(2,1)S(1)} %convolution_convert_fusion.3), channel_id=1, source_target_pairs={{0,1},{1,2},{2,3},{3,4},{4,5},{5,6},{6,7},{7,0},{8,9},{9,10},{10,1... | collective-permute-start | bytes 786440 | tf_op jit(solution)/shard_map/ppermute | solution.py:17
  152.7 10.1 %collective-permute-start.4 = (bf16[512,256]{1,0:T(8,128)(2,1)S(1)}, bf16[512,256]{1,0:T(8,128)(2,1)S(1)}, u32[]{:S(2)}, u32[]{:S(2)}) collective-permute-start(bf16[512,256]{1,0:T(8,128)(2,1)S(1)} %convolution_convert_fusion.2), channel_id=1, source_target_pairs={{0,7},{1,0},{2,1},{3,2},{4,3},{5,4},{6,5},{7,6},{8,15},{9,8},{10,9... | collective-permute-start | bytes 786440 | tf_op jit(solution)/shard_map/ppermute | solution.py:17
  162.7 8.8 %collective-permute-start.1 = (bf16[512,256]{1,0:T(8,128)(2,1)S(1)}, bf16[512,256]{1,0:T(8,128)(2,1)S(1)}, u32[]{:S(2)}, u32[]{:S(2)}) collective-permute-start(bf16[512,256]{1,0:T(8,128)(2,1)S(1)} %add_convert_fusion.10), channel_id=1, source_target_pairs={{0,1},{1,2},{2,3},{3,4},{4,5},{5,6},{6,7},{7,0},{8,9},{9,10},{10,1... | collective-permute-start | bytes 786440 | tf_op jit(solution)/shard_map/ppermute | solution.py:17
  163.3 8.9 %collective-permute-start.5 = (bf16[512,256]{1,0:T(8,128)(2,1)S(1)}, bf16[512,256]{1,0:T(8,128)(2,1)S(1)}, u32[]{:S(2)}, u32[]{:S(2)}) collective-permute-start(bf16[512,256]{1,0:T(8,128)(2,1)S(1)} %add_convert_fusion.7), channel_id=1, source_target_pairs={{0,7},{1,0},{2,1},{3,2},{4,3},{5,4},{6,5},{7,6},{8,15},{9,8},{10,9... | collective-permute-start | bytes 786440 | tf_op jit(solution)/shard_map/ppermute | solution.py:17
  171.6 7.9 %collective-permute-start.2 = (bf16[512,256]{1,0:T(8,128)(2,1)S(1)}, bf16[512,256]{1,0:T(8,128)(2,1)S(1)}, u32[]{:S(2)}, u32[]{:S(2)}) collective-permute-start(bf16[512,256]{1,0:T(8,128)(2,1)S(1)} %add_convert_fusion.9), channel_id=1, source_target_pairs={{0,1},{1,2},{2,3},{3,4},{4,5},{5,6},{6,7},{7,0},{8,9},{9,10},{10,1... | collective-permute-start | bytes 786440 | tf_op jit(solution)/shard_map/ppermute | solution.py:17
  172.3 7.9 %collective-permute-start.6 = (bf16[512,256]{1,0:T(8,128)(2,1)S(1)}, bf16[512,256]{1,0:T(8,128)(2,1)}, u32[]{:S(2)}, u32[]{:S(2)}) collective-permute-start(bf16[512,256]{1,0:T(8,128)(2,1)S(1)} %add_convert_fusion.6), channel_id=1, source_target_pairs={{0,7},{1,0},{2,1},{3,2},{4,3},{5,4},{6,5},{7,6},{8,15},{9,8},{10,9... | collective-permute-start | bytes 786440 | tf_op jit(solution)/shard_map/ppermute | solution.py:17
  179.6 7.8 %collective-permute-start.3 = (bf16[512,256]{1,0:T(8,128)(2,1)S(1)}, bf16[512,256]{1,0:T(8,128)(2,1)}, u32[]{:S(2)}, u32[]{:S(2)}) collective-permute-start(bf16[512,256]{1,0:T(8,128)(2,1)S(1)} %add_convert_fusion.8), channel_id=1, source_target_pairs={{0,1},{1,2},{2,3},{3,4},{4,5},{5,6},{6,7},{7,0},{8,9},{9,10},{10,1... | collective-permute-start | bytes 786440 | tf_op jit(solution)/shard_map/ppermute | solution.py:17
  (7 other events, 69.4 us)
Sparse Core Ops, SparseCore 0:
  9.9 83.3 all-gather.1
